TPU v7x, 32 devices: a whole 2x2x4 slice. The times are simulated.
32 devices in a mesh: pw: 2 (over x), pair: 16 (over z, y, core).
Axes of the slice: x: 2, y: 2, z: 4, core: 2. Of those that a mesh axis runs over, the one named last changes fastest.
Arguments:
- valence_pairs: bfloat16 [64, 64, 8192], P('pair', None, 'pw'), may hold values from -0.59765625 to 0.59765625
- conduction_pairs: bfloat16 [16, 256, 8192], P('pair', None, 'pw'), may hold values from -0.59765625 to 0.59765625
- screening: float32 [8192], P('pw'), may hold values from 0.1 to 2
Outputs:
- kernel: float32 [64, 16, 64, 256], P('pair', None, 'pw')
All inputs are finite; a program needn't handle non-finite values.
Results may differ from a plain program's by a relative error of at most 0.0029.
Values may be sent and summed in bfloat16 or wider, within the bound.
A program may use at most 128 MiB of HBM per device.

v0:
```python
import functools

import jax
import jax.numpy as jnp
from jax import lax
from jax.experimental import pallas as pl
from jax.experimental.pallas import tpu as pltpu
from jax.sharding import PartitionSpec as P

MESH = pl.DeviceIdType.MESH
SIDE = 4
CHUNKS = 16


def contract(piece, flat_right, band_dev, conduction):
    first, second, width = piece.shape
    product = lax.dot_general(
        piece.reshape(first * second, width),
        flat_right,
        (((1,), (1,)), ((), ())),
        preferred_element_type=jnp.float32,
    )
    return product.reshape(first, second, band_dev, conduction)


def general_body(valence_pairs, conduction_pairs, screening):
    screened = (valence_pairs.astype(jnp.float32) * screening[None, None, :]).astype(jnp.bfloat16)
    band_dev, conduction, plane_dev = conduction_pairs.shape
    flat_local = conduction_pairs.reshape(band_dev * conduction, plane_dev)
    partial_value = contract(
        lax.all_gather(screened, "pair", axis=0, tiled=True), flat_local, band_dev, conduction
    )
    terms = lax.psum_scatter(partial_value, "pw", scatter_dimension=1, tiled=True)
    owned = lax.all_to_all(terms, "pair", split_axis=0, concat_axis=2, tiled=True)
    return owned.transpose(0, 2, 1, 3)


def flip(bit, by):
    return bit + by - 2 * bit * by


def grid_kernel(
    val, con, scr_row, out, raw, scr, bb, acc, xs, xr, zs, zr,
    loc, a1s, a1r, a2s, a2r, a3s, a3r, b1s, b1r, b2s, b2r, b3s, b3r, xss, xsr, zss, zsr,
):
    me, x = lax.axis_index("pair"), lax.axis_index("pw")
    core, y, zl, zh = me % 2, (me // 2) % 2, (me // 4) % 2, me // 8
    rows, depth = val.shape
    cols = con.shape[0]
    half = out.shape[2]
    step = rows // CHUNKS
    cstep = cols // CHUNKS

    def at(fc, fy, fl, fh):
        return (x, flip(core, fc) + 2 * flip(y, fy) + 4 * flip(zl, fl) + 8 * flip(zh, fh))

    def remote(src, dst, s, r, dev):
        return pltpu.make_async_remote_copy(
            src_ref=src, dst_ref=dst, send_sem=s, recv_sem=r, device_id=dev, device_id_type=MESH
        )

    def arows(k):
        return pl.ds(pl.multiple_of(k * step, step), step)

    def brows(k):
        return pl.ds(pl.multiple_of(k * cstep, cstep), cstep)

    sibling, beside, near, far = at(1, 0, 0, 0), at(0, 1, 0, 0), at(0, 0, 1, 0), at(0, 0, 0, 1)
    a1 = remote(val, raw.at[1], a1s.at[0], a1r.at[0], sibling)
    b1 = remote(con, bb.at[1], b1s.at[0], b1r.at[0], beside)

    def a2(k):
        return remote(val.at[arows(k)], raw.at[2, arows(k)], a2s.at[k], a2r.at[k], near)

    def b2(k):
        return remote(con.at[brows(k)], bb.at[2, brows(k)], b2s.at[k], b2r.at[k], far)

    def a3(k):
        return remote(raw.at[2, arows(k)], raw.at[3, arows(k)], a3s.at[k], a3r.at[k], sibling)

    def b3(k):
        return remote(bb.at[2, brows(k)], bb.at[3, brows(k)], b3s.at[k], b3r.at[k], beside)

    def xcopy(t):
        return remote(xs.at[t], xr.at[t], xss.at[t], xsr.at[t], (1 - x, me))

    def zcopy(t):
        a = t // SIDE
        return remote(zs.at[t], zr.at[t], zss.at[t], zsr.at[t], at(a % 2, 0, a // 2, 0))

    def each(n, fn, lo=0):
        def run(k, carry):
            fn(k)
            return carry
        lax.fori_loop(lo, n, run, 0)

    barrier = pltpu.get_barrier_semaphore()
    greeted = (sibling, beside, near, far, at(1, 0, 1, 0), (1 - x, me))
    for dev in greeted:
        pl.semaphore_signal(barrier, inc=1, device_id=dev, device_id_type=MESH)
    own_a = pltpu.make_async_copy(val, raw.at[0], loc.at[0])
    own_b = pltpu.make_async_copy(con, bb.at[0], loc.at[1])
    own_a.start()
    own_b.start()
    pl.semaphore_wait(barrier, len(greeted))

    end = zl == zh

    @pl.when(end)
    def _():
        each(CHUNKS, lambda k: a2(k).start())
        each(CHUNKS, lambda k: b2(k).start())

    @pl.when(jnp.logical_not(end))
    def _():
        each(CHUNKS, lambda k: b2(k).start())

    b1.start()
    a1.start()

    def screen(a):
        def part(i):
            r = pl.ds(pl.multiple_of(i * 16, 16), 16)
            scr[a, r, :] = (raw[a, r, :].astype(jnp.float32) * scr_row[...]).astype(jnp.bfloat16)
        each(rows // 16, part)

    vb, w = acc.shape[1], acc.shape[2]

    def owned_c(a, b):
        return flip(core, a % 2) + 2 * flip(y, b % 2) + 4 * flip(zl, a // 2) + 8 * flip(zh, b // 2)

    def group(lo, hi, b):
        def mm(a):
            t = a * SIDE + b
            prod = lax.dot_general(
                scr[a], bb[b], (((1,), (1,)), ((), ())), preferred_element_type=jnp.float32
            )
            acc[t] = prod.reshape(vb, w, cols)
            other = pl.ds(pl.multiple_of((1 - x) * half, half), half)
            xs[t] = acc[t, :, other, :].astype(jnp.bfloat16)
            xcopy(t).start()
        each(hi, mm, lo)

    def drain(lo, hi, b):
        def fin(a):
            t = a * SIDE + b
            xcopy(t).wait_recv()
            mine = pl.ds(pl.multiple_of(x * half, half), half)
            total = acc[t, :, mine, :] + xr[t].astype(jnp.float32)

            @pl.when(a == 0)
            def _():
                out[:, pl.ds(owned_c(0, b), 1), :, :] = total[:, None]

            @pl.when(a > 0)
            def _():
                zs[t] = total.astype(jnp.bfloat16)
                zcopy(t).start()
        each(hi, fin, lo)

    own_a.wait()
    screen(0)
    own_b.wait()
    a1.wait_recv()
    screen(1)
    group(0, 2, 0)

    def pass_a(k):
        a2(k).wait_recv()
        a3(k).start()

    def pass_b(k):
        b2(k).wait_recv()
        b3(k).start()

    def take_a():
        each(CHUNKS, lambda k: a3(k).wait_recv())
        screen(2)
        screen(3)

    @pl.when(end)
    def _():
        each(CHUNKS, pass_b)
        drain(0, 2, 0)
        b1.wait_recv()
        each(3, lambda b: group(0, 2, b), 1)
        each(3, lambda b: drain(0, 2, b), 1)
        each(CHUNKS, pass_a)
        take_a()
        each(3, lambda b: group(2, 4, b))
        each(3, lambda b: drain(2, 4, b))

    @pl.when(jnp.logical_not(end))
    def _():
        each(CHUNKS, pass_a)
        each(CHUNKS, lambda k: b2(k).wait_send())
        each(CHUNKS, lambda k: a2(k).start())
        drain(0, 2, 0)
        take_a()
        group(2, 4, 0)
        b1.wait_recv()
        group(0, 4, 1)
        drain(2, 4, 0)
        drain(0, 4, 1)
        each(CHUNKS, pass_b)
        group(0, 4, 2)
        drain(0, 4, 2)

    each(CHUNKS, lambda k: b3(k).wait_recv())
    group(0, 4, 3)
    drain(0, 4, 3)

    def land(t):
        zcopy(t).wait_recv()
        c = owned_c(t // SIDE, t % SIDE)
        out[:, pl.ds(c, 1), :, :] = zr[t].astype(jnp.float32)[:, None]
    each(SIDE * SIDE, land, SIDE)

    a1.wait_send()
    b1.wait_send()

    def sent(k):
        a2(k).wait_send()
        a3(k).wait_send()
        b3(k).wait_send()
    each(CHUNKS, sent)

    @pl.when(end)
    def _():
        each(CHUNKS, lambda k: b2(k).wait_send())
    each(SIDE * SIDE, lambda t: xcopy(t).wait_send())
    each(SIDE * SIDE, lambda t: zcopy(t).wait_send(), SIDE)


def grid_body(valence_pairs, conduction_pairs, screening):
    vb, w, depth = valence_pairs.shape
    bands, conduction, _ = conduction_pairs.shape
    cols = bands * conduction
    rows = vb * w
    half = w // lax.axis_size("pw")
    total_c = bands * lax.axis_size("pair")
    tiles = SIDE * SIDE
    dma = pltpu.SemaphoreType.DMA
    bf16 = jnp.bfloat16
    return pl.pallas_call(
        grid_kernel,
        out_shape=jax.ShapeDtypeStruct((vb, total_c, half, conduction), jnp.float32),
        in_specs=[
            pl.BlockSpec(memory_space=pl.ANY),
            pl.BlockSpec(memory_space=pl.ANY),
            pl.BlockSpec(memory_space=pltpu.VMEM),
        ],
        out_specs=pl.BlockSpec(memory_space=pltpu.VMEM),
        scratch_shapes=[
            pltpu.VMEM((SIDE, rows, depth), bf16),
            pltpu.VMEM((SIDE, rows, depth), bf16),
            pltpu.VMEM((SIDE, cols, depth), bf16),
            pltpu.VMEM((tiles, vb, w, cols), jnp.float32),
            pltpu.VMEM((tiles, vb, half, cols), bf16),
            pltpu.VMEM((tiles, vb, half, cols), bf16),
            pltpu.VMEM((tiles, vb, half, cols), bf16),
            pltpu.VMEM((tiles, vb, half, cols), bf16),
            dma((2,)),
            dma((1,)), dma((1,)),
            dma((CHUNKS,)), dma((CHUNKS,)), dma((CHUNKS,)), dma((CHUNKS,)),
            dma((1,)), dma((1,)),
            dma((CHUNKS,)), dma((CHUNKS,)), dma((CHUNKS,)), dma((CHUNKS,)),
            dma((tiles,)), dma((tiles,)), dma((tiles,)), dma((tiles,)),
        ],
        compiler_params=pltpu.CompilerParams(
            collective_id=0, has_side_effects=True, vmem_limit_bytes=56 * 1024 * 1024
        ),
    )(
        valence_pairs.reshape(rows, depth),
        conduction_pairs.reshape(cols, depth),
        screening.reshape(1, depth),
    )


def solution(mesh):
    placed = (P("pair", None, "pw"), P("pair", None, "pw"), P("pw"))
    squared = mesh.shape["pw"] == 2 and mesh.shape["pair"] == SIDE * SIDE

    def body(valence_pairs, conduction_pairs, screening):
        if squared and conduction_pairs.shape[0] == 1:
            return grid_body(valence_pairs, conduction_pairs, screening)
        return general_body(valence_pairs, conduction_pairs, screening)

    return jax.shard_map(
        body, mesh=mesh, in_specs=placed, out_specs=P("pair", None, "pw", None), check_vma=False
    )
```

profile of v0, /device:TPU:0, one launch (start us, length us, event | category | flops | bytes accessed | tf_op | source)
XLA Modules:
  0.0 130.4 jit_solution(17207500766257402981)
XLA Ops:
  0.0 127.3 %shard_map.37 = f32[4,16,32,256]{3,2,1,0:T(8,128)} custom-call(bf16[256,4096]{1,0:T(8,128)(2,1)} %bitcast.3, bf16[256,4096]{1,0:T(8,128)(2,1)} %bitcast.4, f32[1,4096]{1,0:T(1,128)} %bitcast.5), custom_call_target="tpu_custom_call" | custom-call | tf_op jit(solution)/shard_map/pallas_call | solution.py:245
  127.3 3.2 %copy.5 = f32[4,16,32,256]{3,2,1,0:T(8,128)} copy(f32[4,16,32,256]{3,2,1,0:T(8,128)} %shard_map.37) | data formatting | bytes 4194304
where the time goes:
time: 133 us; the launch traced here: 130 us
  Pallas kernels  127 us (95%)
  local copies, waits for them, and re-layouts  3.16 us (2%)
    pallas_call x1, Pallas kernels, grid_body(): pl.pallas_call(grid_kernel, out_shape=jax.ShapeDtypeStruct((vb, total_c,...  127 us
    unnamed x1, local copies, waits for them, and re-layouts  3.16 us

commit v1 on v0

v1 whole, which is shorter than its diff:
```python
import functools

import jax
import jax.numpy as jnp
from jax import lax
from jax.experimental import pallas as pl
from jax.experimental.pallas import tpu as pltpu
from jax.sharding import PartitionSpec as P

MESH = pl.DeviceIdType.MESH
SIDE = 4
CHUNKS = 16
BLOCKS = 5
PARTS = 2


def contract(piece, flat_right, band_dev, conduction):
    first, second, width = piece.shape
    product = lax.dot_general(
        piece.reshape(first * second, width),
        flat_right,
        (((1,), (1,)), ((), ())),
        preferred_element_type=jnp.float32,
    )
    return product.reshape(first, second, band_dev, conduction)


def general_body(valence_pairs, conduction_pairs, screening):
    screened = (valence_pairs.astype(jnp.float32) * screening[None, None, :]).astype(jnp.bfloat16)
    band_dev, conduction, plane_dev = conduction_pairs.shape
    flat_local = conduction_pairs.reshape(band_dev * conduction, plane_dev)
    partial_value = contract(
        lax.all_gather(screened, "pair", axis=0, tiled=True), flat_local, band_dev, conduction
    )
    terms = lax.psum_scatter(partial_value, "pw", scatter_dimension=1, tiled=True)
    owned = lax.all_to_all(terms, "pair", split_axis=0, concat_axis=2, tiled=True)
    return owned.transpose(0, 2, 1, 3)


def flip(bit, by):
    return bit + by - 2 * bit * by


def grid_kernel(
    val, con, scr_row, out, raw, scr, bb, acc, xs, xr, zs, zr,
    loc, a1s, a1r, a2s, a2r, a3s, a3r, b1s, b1r, b2s, b2r, b3s, b3r, b4s, b4r, xss, xsr, zss, zsr,
):
    me, x = lax.axis_index("pair"), lax.axis_index("pw")
    core, y, zl, zh = me % 2, (me // 2) % 2, (me // 4) % 2, me // 8
    rows, depth = val.shape
    cols = con.shape[0]
    half = out.shape[2]
    vb, w, part = acc.shape[1], acc.shape[2], acc.shape[3]
    step = rows // CHUNKS
    cstep = cols // CHUNKS
    end = zl == zh
    mid = zl != zh

    def at(fc, fy, fl, fh):
        return (x, flip(core, fc) + 2 * flip(y, fy) + 4 * flip(zl, fl) + 8 * flip(zh, fh))

    def remote(src, dst, s, r, dev):
        return pltpu.make_async_remote_copy(
            src_ref=src, dst_ref=dst, send_sem=s, recv_sem=r, device_id=dev, device_id_type=MESH
        )

    def arows(k):
        return pl.ds(pl.multiple_of(k * step, step), step)

    def brows(k):
        return pl.ds(pl.multiple_of(k * cstep, cstep), cstep)

    sibling, beside, near, far = at(1, 0, 0, 0), at(0, 1, 0, 0), at(0, 0, 1, 0), at(0, 0, 0, 1)
    across = at(0, 0, 1, 1)
    a1 = remote(raw.at[0], raw.at[1], a1s.at[0], a1r.at[0], sibling)
    b1 = remote(bb.at[0], bb.at[1], b1s.at[0], b1r.at[0], beside)

    def a2(k):
        return remote(raw.at[0, arows(k)], raw.at[2, arows(k)], a2s.at[k], a2r.at[k], near)

    def a3(k):
        return remote(raw.at[2, arows(k)], raw.at[3, arows(k)], a3s.at[k], a3r.at[k], sibling)

    def b2(k):
        return remote(bb.at[0, brows(k)], bb.at[2, brows(k)], b2s.at[k], b2r.at[k], far)

    def b2pass(k):
        return remote(bb.at[4, brows(k)], bb.at[2, brows(k)], b2s.at[k], b2r.at[k], near)

    def b3(k):
        return remote(bb.at[2, brows(k)], bb.at[3, brows(k)], b3s.at[k], b3r.at[k], beside)

    def b4(k):
        return remote(bb.at[0, brows(k)], bb.at[4, brows(k)], b4s.at[k], b4r.at[k], across)

    def slot(a, b, h):
        return (b * SIDE + a) * PARTS + h

    def xcopy(t):
        return remote(xs.at[t], xr.at[t], xss.at[t], xsr.at[t], (1 - x, me))

    def zcopy(t, a):
        return remote(zs.at[t], zr.at[t], zss.at[t], zsr.at[t], at(a % 2, 0, a // 2, 0))

    def each(n, fn, lo=0):
        def run(k, carry):
            fn(k)
            return carry
        lax.fori_loop(lo, n, run, 0)

    def active(a, b):
        kept = jnp.logical_and(b == 4, jnp.logical_and(mid, a < 2))
        shared = jnp.logical_and(b == 2, jnp.logical_or(mid, a < 2))
        return jnp.logical_or(jnp.logical_or(kept, shared), jnp.logical_and(b != 2, b != 4))

    def returned(a, b):
        kept = jnp.logical_and(b == 4, jnp.logical_and(mid, a < 2))
        shared = jnp.logical_and(b == 2, jnp.logical_or(end, a < 2))
        return jnp.logical_or(jnp.logical_or(kept, shared), jnp.logical_and(b != 2, b != 4))

    def owner(a, b):
        fy = jnp.where(b == 4, 0, b % 2)
        fl = jnp.where(b == 4, 1, 0)
        fh = jnp.where(b >= 2, 1, 0)
        return (
            flip(core, a % 2) + 2 * flip(y, fy) + 4 * flip(flip(zl, a // 2), fl) + 8 * flip(zh, fh)
        )

    barrier = pltpu.get_barrier_semaphore()
    greeted = (sibling, beside, near, far, at(1, 0, 1, 0), (1 - x, me), across)
    for dev in greeted:
        pl.semaphore_signal(barrier, inc=1, device_id=dev, device_id_type=MESH)
    own_a = pltpu.make_async_copy(val, raw.at[0], loc.at[0])
    own_b = pltpu.make_async_copy(con, bb.at[0], loc.at[1])
    own_a.start()
    own_b.start()
    own_a.wait()
    own_b.wait()
    pl.semaphore_wait(barrier, len(greeted))

    @pl.when(mid)
    def _():
        each(CHUNKS, lambda k: b4(k).start())

    each(CHUNKS, lambda k: a2(k).start())

    @pl.when(end)
    def _():
        each(CHUNKS, lambda k: b2(k).start())

    b1.start()
    a1.start()

    lines = 16

    def screen(a, r):
        scr[a, r, :] = (raw[a, r, :].astype(jnp.float32) * scr_row[...]).astype(jnp.bfloat16)

    def screen_all(a):
        each(rows // lines, lambda i: screen(a, pl.ds(pl.multiple_of(i * lines, lines), lines)))

    def compute(a, b, h):
        @pl.when(active(a, b))
        def _():
            t = slot(a, b, h)
            right = bb[b, pl.ds(pl.multiple_of(h * part, part), part), :]
            prod = lax.dot_general(
                scr[a], right, (((1,), (1,)), ((), ())), preferred_element_type=jnp.float32
            )
            acc[t] = prod.reshape(vb, w, part)
            other = pl.ds(pl.multiple_of((1 - x) * half, half), half)
            xs[t] = acc[t, :, other, :].astype(jnp.bfloat16)
            xcopy(t).start()

    def place(a, b, h, value):
        lanes = pl.ds(pl.multiple_of(h * part, part), part)
        out[:, pl.ds(owner(a, b), 1), :, lanes] = value[:, None]

    def drain(a, b, h):
        @pl.when(active(a, b))
        def _():
            t = slot(a, b, h)
            xcopy(t).wait_recv()
            mine = pl.ds(pl.multiple_of(x * half, half), half)
            total = acc[t, :, mine, :] + xr[t].astype(jnp.float32)

            @pl.when(a == 0)
            def _():
                place(0, b, h, total)

            @pl.when(a > 0)
            def _():
                zs[t] = total.astype(jnp.bfloat16)
                zcopy(t, a).start()

    def land(a, b, h):
        @pl.when(returned(a, b))
        def _():
            t = slot(a, b, h)
            zcopy(t, a).wait_recv()
            place(a, b, h, zr[t].astype(jnp.float32))

    screen_all(0)
    each(PARTS, lambda h: compute(0, 0, h))
    a1.wait_recv()
    screen_all(1)
    each(PARTS, lambda h: compute(1, 0, h))

    def first(k):
        @pl.when(mid)
        def _():
            b4(k).wait_recv()
            b2pass(k).start()

        a2(k).wait_recv()
        a3(k).start()
        screen(2, arows(k))

        @pl.when(k > 0)
        def _():
            a3(k - 1).wait_recv()
            screen(3, arows(k - 1))

    each(CHUNKS, first)
    a3(CHUNKS - 1).wait_recv()
    screen(3, arows(CHUNKS - 1))
    each(PARTS * 2, lambda i: drain(1 - i // PARTS, 0, i % PARTS))
    b1.wait_recv()

    turns = CHUNKS // 2

    def early(i):
        j = i - 2
        a = jnp.where(i < 2, i, jnp.where(j < 2, 2 + j, j - 2))
        b = jnp.where(i < 2, 4, jnp.where(j < 2, 0, 1))
        return a, b

    def relay(k):
        b2(k).wait_recv()
        b3(k).start()

    def second(k):
        relay(k)
        a, b = early(k)
        each(PARTS, lambda h: compute(a, b, h))

        @pl.when(k > 0)
        def _():
            pa, pb = early(k - 1)
            each(PARTS, lambda h: drain(pa, pb, h))

    each(turns, second)

    def late(i):
        return SIDE - 1 - i % SIDE, 2 + i // SIDE

    def third(k):
        relay(k + turns)

        @pl.when(k == 0)
        def _():
            pa, pb = early(turns - 1)
            each(PARTS, lambda h: drain(pa, pb, h))

        @pl.when(k == SIDE)
        def _():
            each(turns, lambda i: b3(i).wait_recv())

        a, b = late(k)
        compute(a, b, 0)

        @pl.when(k > 0)
        def _():
            pa, pb = late(k - 1)
            drain(pa, pb, 0)

    each(turns, third)

    def last(k):
        @pl.when(k == SIDE)
        def _():
            each(CHUNKS, lambda i: b3(i).wait_recv(), turns)

        a, b = late(k)
        compute(a, b, 1)

        @pl.when(k == 0)
        def _():
            pa, pb = late(turns - 1)
            drain(pa, pb, 0)

        @pl.when(k > 1)
        def _():
            pa, pb = late(k - 2)
            drain(pa, pb, 1)

    each(turns, last)

    def finish(k):
        pa, pb = late(k)
        drain(pa, pb, 1)

    each(turns, finish, turns - 2)

    def arrive(i):
        h = i // (BLOCKS * (SIDE - 1))
        j = i % (BLOCKS * (SIDE - 1))
        land(1 + j % (SIDE - 1), j // (SIDE - 1), h)

    each(PARTS * BLOCKS * (SIDE - 1), arrive)

    a1.wait_send()
    b1.wait_send()

    def sent(k):
        a2(k).wait_send()
        a3(k).wait_send()
        b2(k).wait_send()
        b3(k).wait_send()

        @pl.when(mid)
        def _():
            b4(k).wait_send()
    each(CHUNKS, sent)

    def passed(i):
        a, b, h = (i // PARTS) % SIDE, i // (PARTS * SIDE), i % PARTS

        @pl.when(active(a, b))
        def _():
            xcopy(i).wait_send()

            @pl.when(a > 0)
            def _():
                zcopy(i, a).wait_send()
    each(BLOCKS * SIDE * PARTS, passed)


def grid_body(valence_pairs, conduction_pairs, screening):
    vb, w, depth = valence_pairs.shape
    bands, conduction, _ = conduction_pairs.shape
    cols = bands * conduction
    rows = vb * w
    half = w // lax.axis_size("pw")
    total_c = bands * lax.axis_size("pair")
    tiles = BLOCKS * SIDE * PARTS
    part = cols // PARTS
    dma = pltpu.SemaphoreType.DMA
    bf16 = jnp.bfloat16
    return pl.pallas_call(
        grid_kernel,
        out_shape=jax.ShapeDtypeStruct((vb, total_c, half, conduction), jnp.float32),
        in_specs=[
            pl.BlockSpec(memory_space=pl.ANY),
            pl.BlockSpec(memory_space=pl.ANY),
            pl.BlockSpec(memory_space=pltpu.VMEM),
        ],
        out_specs=pl.BlockSpec(memory_space=pltpu.VMEM),
        scratch_shapes=[
            pltpu.VMEM((SIDE, rows, depth), bf16),
            pltpu.VMEM((SIDE, rows, depth), bf16),
            pltpu.VMEM((BLOCKS, cols, depth), bf16),
            pltpu.VMEM((tiles, vb, w, part), jnp.float32),
            pltpu.VMEM((tiles, vb, half, part), bf16),
            pltpu.VMEM((tiles, vb, half, part), bf16),
            pltpu.VMEM((tiles, vb, half, part), bf16),
            pltpu.VMEM((tiles, vb, half, part), bf16),
            dma((2,)),
            dma((1,)), dma((1,)),
            dma((CHUNKS,)), dma((CHUNKS,)), dma((CHUNKS,)), dma((CHUNKS,)),
            dma((1,)), dma((1,)),
            dma((CHUNKS,)), dma((CHUNKS,)), dma((CHUNKS,)), dma((CHUNKS,)),
            dma((CHUNKS,)), dma((CHUNKS,)),
            dma((tiles,)), dma((tiles,)), dma((tiles,)), dma((tiles,)),
        ],
        compiler_params=pltpu.CompilerParams(
            collective_id=0, has_side_effects=True, vmem_limit_bytes=56 * 1024 * 1024
        ),
    )(
        valence_pairs.reshape(rows, depth),
        conduction_pairs.reshape(cols, depth),
        screening.reshape(1, depth),
    )


def solution(mesh):
    placed = (P("pair", None, "pw"), P("pair", None, "pw"), P("pw"))
    squared = mesh.shape["pw"] == 2 and mesh.shape["pair"] == SIDE * SIDE

    def body(valence_pairs, conduction_pairs, screening):
        if squared and conduction_pairs.shape[0] == 1:
            return grid_body(valence_pairs, conduction_pairs, screening)
        return general_body(valence_pairs, conduction_pairs, screening)

    return jax.shard_map(
        body, mesh=mesh, in_specs=placed, out_specs=P("pair", None, "pw", None), check_vma=False
    )
```

time: 133 us -> 123 us (0.925); the launches traced: 130 us -> 123 us
  Pallas kernels: 127 us -> 120 us
    pallas_call x1, Pallas kernels: 127 us -> 120 us  [grid_body(): pl.pallas_call(grid_kernel, out_shape=jax.ShapeDtypeStruct((vb, total_c,...]
where the time goes in v1:
time: 123 us
  Pallas kernels  120 us (98%)
  local copies, waits for them, and re-layouts  3.16 us (3%)
    pallas_call x1, Pallas kernels, grid_body(): pl.pallas_call(grid_kernel, out_shape=jax.ShapeDtypeStruct((vb, total_c,...  120 us
    unnamed x1, local copies, waits for them, and re-layouts  3.16 us

profile of v1, /device:TPU:0, one launch (start us, length us, event | category | flops | bytes accessed | tf_op | source)
XLA Modules:
  0.0 123.0 jit_solution(13508713196087862003)
XLA Ops:
  0.0 119.9 %shard_map.37 = f32[4,16,32,256]{3,2,1,0:T(8,128)} custom-call(bf16[256,4096]{1,0:T(8,128)(2,1)} %bitcast.3, bf16[256,4096]{1,0:T(8,128)(2,1)} %bitcast.4, f32[1,4096]{1,0:T(1,128)} %bitcast.5), custom_call_target="tpu_custom_call" | custom-call | tf_op jit(solution)/shard_map/pallas_call | solution.py:350
  119.9 3.2 %copy.5 = f32[4,16,32,256]{3,2,1,0:T(8,128)} copy(f32[4,16,32,256]{3,2,1,0:T(8,128)} %shard_map.37) | data formatting | bytes 4194304

commit v2 on v1

--- a/solution.py
+++ b/solution.py
@@ -9,8 +9,9 @@
 
 MESH = pl.DeviceIdType.MESH
 SIDE = 4
-CHUNKS = 16
+CHUNKS = 8
 BLOCKS = 5
+CUTS = 8
 PARTS = 2
 
 
@@ -43,7 +44,7 @@
 
 def grid_kernel(
     val, con, scr_row, out, raw, scr, bb, acc, xs, xr, zs, zr,
-    loc, a1s, a1r, a2s, a2r, a3s, a3r, b1s, b1r, b2s, b2r, b3s, b3r, b4s, b4r, xss, xsr, zss, zsr,
+    loc, a1s, a1r, a2s, a2r, a3s, a3r, b1s, b1r, b2s, b2r, b3s, b3r, b4s, b4r, gate, xss, xsr, zss, zsr,
 ):
     me, x = lax.axis_index("pair"), lax.axis_index("pw")
     core, y, zl, zh = me % 2, (me // 2) % 2, (me // 4) % 2, me // 8
@@ -53,6 +54,8 @@
     vb, w, part = acc.shape[1], acc.shape[2], acc.shape[3]
     step = rows // CHUNKS
     cstep = cols // CHUNKS
+    cut = depth // CUTS
+    bits = PARTS * CUTS
     end = zl == zh
     mid = zl != zh
 
@@ -70,10 +73,12 @@
     def brows(k):
         return pl.ds(pl.multiple_of(k * cstep, cstep), cstep)
 
-    sibling, beside, near, far = at(1, 0, 0, 0), at(0, 1, 0, 0), at(0, 0, 1, 0), at(0, 0, 0, 1)
-    across = at(0, 0, 1, 1)
+    sibling, beside, near = at(1, 0, 0, 0), at(0, 1, 0, 0), at(0, 0, 1, 0)
+    far, across = at(0, 0, 0, 1), at(0, 0, 1, 1)
     a1 = remote(raw.at[0], raw.at[1], a1s.at[0], a1r.at[0], sibling)
-    b1 = remote(bb.at[0], bb.at[1], b1s.at[0], b1r.at[0], beside)
+
+    def b1(k):
+        return remote(bb.at[0, brows(k)], bb.at[1, brows(k)], b1s.at[k], b1r.at[k], beside)
 
     def a2(k):
         return remote(raw.at[0, arows(k)], raw.at[2, arows(k)], a2s.at[k], a2r.at[k], near)
@@ -81,14 +86,19 @@
     def a3(k):
         return remote(raw.at[2, arows(k)], raw.at[3, arows(k)], a3s.at[k], a3r.at[k], sibling)
 
+    def bit(b, k):
+        lines = pl.ds(pl.multiple_of((k // CUTS) * part, part), part)
+        lanes = pl.ds(pl.multiple_of((k % CUTS) * cut, cut), cut)
+        return bb.at[b, lines, lanes]
+
     def b2(k):
-        return remote(bb.at[0, brows(k)], bb.at[2, brows(k)], b2s.at[k], b2r.at[k], far)
+        return remote(bit(0, k), bit(2, k), b2s.at[k], b2r.at[k], far)
 
     def b2pass(k):
-        return remote(bb.at[4, brows(k)], bb.at[2, brows(k)], b2s.at[k], b2r.at[k], near)
+        return remote(bit(4, k), bit(2, k), b2s.at[k], b2r.at[k], near)
 
     def b3(k):
-        return remote(bb.at[2, brows(k)], bb.at[3, brows(k)], b3s.at[k], b3r.at[k], beside)
+        return remote(bit(2, k), bit(3, k), b3s.at[k], b3r.at[k], beside)
 
     def b4(k):
         return remote(bb.at[0, brows(k)], bb.at[4, brows(k)], b4s.at[k], b4r.at[k], across)
@@ -126,8 +136,24 @@
             flip(core, a % 2) + 2 * flip(y, fy) + 4 * flip(flip(zl, a // 2), fl) + 8 * flip(zh, fh)
         )
 
+    lines = 16
+
+    def screen(a, r):
+        scr[a, r, :] = (raw[a, r, :].astype(jnp.float32) * scr_row[...]).astype(jnp.bfloat16)
+
+    def blank(t):
+        acc[t] = jnp.zeros((vb, w, part), jnp.float32)
+
+    def screen_all(a):
+        each(rows // lines, lambda i: screen(a, pl.ds(pl.multiple_of(i * lines, lines), lines)))
+
     barrier = pltpu.get_barrier_semaphore()
-    greeted = (sibling, beside, near, far, at(1, 0, 1, 0), (1 - x, me), across)
+    greeted = (near, beside, (1 - x, me), sibling)
+
+    @pl.when(mid)
+    def _():
+        pl.semaphore_signal(barrier, inc=1, device_id=across, device_id_type=MESH)
+
     for dev in greeted:
         pl.semaphore_signal(barrier, inc=1, device_id=dev, device_id_type=MESH)
     own_a = pltpu.make_async_copy(val, raw.at[0], loc.at[0])
@@ -135,8 +161,10 @@
     own_a.start()
     own_b.start()
     own_a.wait()
+    screen_all(0)
     own_b.wait()
-    pl.semaphore_wait(barrier, len(greeted))
+    each(2 * SIDE * PARTS, lambda i: blank(2 * SIDE * PARTS + i))
+    pl.semaphore_wait(barrier, len(greeted) + jnp.where(mid, 1, 0))
 
     @pl.when(mid)
     def _():
@@ -144,33 +172,49 @@
 
     each(CHUNKS, lambda k: a2(k).start())
 
-    @pl.when(end)
-    def _():
-        each(CHUNKS, lambda k: b2(k).start())
-
-    b1.start()
+    each(CHUNKS, lambda k: b1(k).start())
     a1.start()
 
-    lines = 16
-
-    def screen(a, r):
-        scr[a, r, :] = (raw[a, r, :].astype(jnp.float32) * scr_row[...]).astype(jnp.bfloat16)
-
-    def screen_all(a):
-        each(rows // lines, lambda i: screen(a, pl.ds(pl.multiple_of(i * lines, lines), lines)))
-
-    def compute(a, b, h):
+    def send(a, b, h):
         @pl.when(active(a, b))
         def _():
             t = slot(a, b, h)
-            right = bb[b, pl.ds(pl.multiple_of(h * part, part), part), :]
-            prod = lax.dot_general(
-                scr[a], right, (((1,), (1,)), ((), ())), preferred_element_type=jnp.float32
-            )
-            acc[t] = prod.reshape(vb, w, part)
             other = pl.ds(pl.multiple_of((1 - x) * half, half), half)
             xs[t] = acc[t, :, other, :].astype(jnp.bfloat16)
             xcopy(t).start()
+
+    def whole(a, b):
+        @pl.when(active(a, b))
+        def _():
+            prod = lax.dot_general(
+                scr[a], bb[b], (((1,), (1,)), ((), ())), preferred_element_type=jnp.float32
+            )
+            for h in range(PARTS):
+                acc[slot(a, b, h)] = prod[:, h * part:(h + 1) * part].reshape(vb, w, part)
+        each(PARTS, lambda h: send(a, b, h))
+
+    def grow(b, k):
+        h, q = k // CUTS, k % CUTS
+        lanes = pl.ds(pl.multiple_of(q * cut, cut), cut)
+        lines = pl.ds(pl.multiple_of(h * part, part), part)
+
+        def one(i):
+            a = SIDE - 1 - i
+
+            @pl.when(active(a, b))
+            def _():
+                prod = lax.dot_general(
+                    scr[a, :, lanes], bb[b, lines, lanes],
+                    (((1,), (1,)), ((), ())), preferred_element_type=jnp.float32,
+                )
+                t = slot(a, b, h)
+                acc[t] = acc[t] + prod.reshape(vb, w, part)
+
+            @pl.when(q == CUTS - 1)
+            def _():
+                send(a, b, h)
+
+        each(SIDE, one)
 
     def place(a, b, h, value):
         lanes = pl.ds(pl.multiple_of(h * part, part), part)
@@ -200,20 +244,36 @@
             zcopy(t, a).wait_recv()
             place(a, b, h, zr[t].astype(jnp.float32))
 
-    screen_all(0)
-    each(PARTS, lambda h: compute(0, 0, h))
+    whole(0, 0)
     a1.wait_recv()
     screen_all(1)
-    each(PARTS, lambda h: compute(1, 0, h))
+    whole(1, 0)
+
+    ready = CHUNKS // PARTS
 
     def first(k):
-        @pl.when(mid)
-        def _():
-            b4(k).wait_recv()
-            b2pass(k).start()
+        @pl.when(jnp.logical_and(mid, k == CHUNKS - 1))
+        def _():
+            each(CHUNKS, lambda i: b4(i).wait_send())
+            for dev in (near, at(1, 0, 1, 0)):
+                pl.semaphore_signal(gate, inc=1, device_id=dev, device_id_type=MESH)
+
+        @pl.when(jnp.logical_and(end, k == CHUNKS - 1))
+        def _():
+            pl.semaphore_wait(gate, 2)
+            each(bits, lambda i: b2(i).start())
 
         a2(k).wait_recv()
         a3(k).start()
+
+        @pl.when(mid)
+        def _():
+            b4(k).wait_recv()
+
+            @pl.when(k % ready == ready - 1)
+            def _():
+                each(CUTS, lambda i: b2pass((k // ready) * CUTS + i).start())
+
         screen(2, arows(k))
 
         @pl.when(k > 0)
@@ -225,9 +285,10 @@
     a3(CHUNKS - 1).wait_recv()
     screen(3, arows(CHUNKS - 1))
     each(PARTS * 2, lambda i: drain(1 - i // PARTS, 0, i % PARTS))
-    b1.wait_recv()
-
-    turns = CHUNKS // 2
+    each(CHUNKS, lambda k: b1(k).wait_recv())
+
+    turns = 2 * SIDE
+    lag = 2
 
     def early(i):
         j = i - 2
@@ -235,93 +296,76 @@
         b = jnp.where(i < 2, 4, jnp.where(j < 2, 0, 1))
         return a, b
 
-    def relay(k):
+    def between(lo, k, hi):
+        return jnp.logical_and(k >= lo, k < hi)
+
+    def tail(k):
+        b3(k).wait_recv()
+        grow(3, k)
+
+    def second(k):
         b2(k).wait_recv()
         b3(k).start()
-
-    def second(k):
-        relay(k)
-        a, b = early(k)
-        each(PARTS, lambda h: compute(a, b, h))
-
-        @pl.when(k > 0)
-        def _():
-            pa, pb = early(k - 1)
-            each(PARTS, lambda h: drain(pa, pb, h))
-
-    each(turns, second)
-
-    def late(i):
-        return SIDE - 1 - i % SIDE, 2 + i // SIDE
-
-    def third(k):
-        relay(k + turns)
-
-        @pl.when(k == 0)
-        def _():
-            pa, pb = early(turns - 1)
-            each(PARTS, lambda h: drain(pa, pb, h))
-
-        @pl.when(k == SIDE)
-        def _():
-            each(turns, lambda i: b3(i).wait_recv())
-
-        a, b = late(k)
-        compute(a, b, 0)
-
-        @pl.when(k > 0)
-        def _():
-            pa, pb = late(k - 1)
-            drain(pa, pb, 0)
-
-    each(turns, third)
-
-    def last(k):
-        @pl.when(k == SIDE)
-        def _():
-            each(CHUNKS, lambda i: b3(i).wait_recv(), turns)
-
-        a, b = late(k)
-        compute(a, b, 1)
-
-        @pl.when(k == 0)
-        def _():
-            pa, pb = late(turns - 1)
-            drain(pa, pb, 0)
-
-        @pl.when(k > 1)
-        def _():
-            pa, pb = late(k - 2)
-            drain(pa, pb, 1)
-
-    each(turns, last)
-
-    def finish(k):
-        pa, pb = late(k)
-        drain(pa, pb, 1)
-
-    each(turns, finish, turns - 2)
-
-    def arrive(i):
-        h = i // (BLOCKS * (SIDE - 1))
-        j = i % (BLOCKS * (SIDE - 1))
-        land(1 + j % (SIDE - 1), j // (SIDE - 1), h)
-
-    each(PARTS * BLOCKS * (SIDE - 1), arrive)
+        grow(2, k)
+
+        @pl.when(k < turns)
+        def _():
+            whole(*early(k))
+
+        @pl.when(k >= lag)
+        def _():
+            tail(k - lag)
+
+        @pl.when(between(lag, k, turns + lag))
+        def _():
+            a, b = early(k - lag)
+            each(PARTS, lambda h: drain(a, b, h))
+
+        @pl.when(between(CUTS + lag, k, CUTS + lag + SIDE))
+        def _():
+            drain(SIDE - 1 - (k - CUTS - lag), 2, 0)
+
+        @pl.when(k >= bits - SIDE)
+        def _():
+            drain(bits - 1 - k, 3, 0)
+
+        @pl.when(k >= bits - 6)
+        def _():
+            i = k - bits + 6
+            land(1, jnp.where(i < 4, i // 2, 4), i % 2)
+
+    each(bits, second)
+    tail(bits - 2)
+    each(SIDE, lambda i: drain(SIDE - 1 - i, 2, 1))
+    tail(bits - 1)
+
+    def arrive(lo, h):
+        def one(j):
+            land(2 + j % 2, lo + j // 2, h)
+        return one
+
+    land(1, 2, 0)
+    land(1, 3, 0)
+    each(4, arrive(0, 0))
+    each(4, arrive(0, 1))
+    each(4, arrive(2, 0))
+    each(SIDE, lambda i: drain(SIDE - 1 - i, 3, 1))
+    land(1, 2, 1)
+    each(4, arrive(2, 1))
+    land(1, 3, 1)
 
     a1.wait_send()
-    b1.wait_send()
 
     def sent(k):
         a2(k).wait_send()
         a3(k).wait_send()
+        b1(k).wait_send()
+    each(CHUNKS, sent)
+
+    def cleared(k):
         b2(k).wait_send()
         b3(k).wait_send()
-
-        @pl.when(mid)
-        def _():
-            b4(k).wait_send()
-    each(CHUNKS, sent)
+    each(bits, cleared)
 
     def passed(i):
         a, b, h = (i // PARTS) % SIDE, i // (PARTS * SIDE), i % PARTS
@@ -345,11 +389,12 @@
     total_c = bands * lax.axis_size("pair")
     tiles = BLOCKS * SIDE * PARTS
     part = cols // PARTS
+    bits = PARTS * CUTS
     dma = pltpu.SemaphoreType.DMA
     bf16 = jnp.bfloat16
     return pl.pallas_call(
         grid_kernel,
-        out_shape=jax.ShapeDtypeStruct((vb, total_c, half, conduction), jnp.float32),
+        out_shape=pltpu.VMEM((vb, total_c, half, conduction), jnp.float32),
         in_specs=[
             pl.BlockSpec(memory_space=pl.ANY),
             pl.BlockSpec(memory_space=pl.ANY),
@@ -368,9 +413,10 @@
             dma((2,)),
             dma((1,)), dma((1,)),
             dma((CHUNKS,)), dma((CHUNKS,)), dma((CHUNKS,)), dma((CHUNKS,)),
-            dma((1,)), dma((1,)),
-            dma((CHUNKS,)), dma((CHUNKS,)), dma((CHUNKS,)), dma((CHUNKS,)),
             dma((CHUNKS,)), dma((CHUNKS,)),
+            dma((bits,)), dma((bits,)), dma((bits,)), dma((bits,)),
+            dma((CHUNKS,)), dma((CHUNKS,)),
+            pltpu.SemaphoreType.REGULAR,
             dma((tiles,)), dma((tiles,)), dma((tiles,)), dma((tiles,)),
         ],
         compiler_params=pltpu.CompilerParams(

time: 123 us -> 117 us (0.951)
  Pallas kernels: 120 us -> 115 us
  local copies, waits for them, and re-layouts: 3.16 us -> 1.32 us
    pallas_call x1, Pallas kernels: 120 us -> 115 us  [grid_body(): pl.pallas_call(grid_kernel, out_shape=pltpu.VMEM((vb, total_c, half, cond...]
    unnamed x1, local copies, waits for them, and re-layouts: 3.16 us -> 1.32 us
where the time goes in v2:
time: 117 us; the launch traced here: 116 us
  Pallas kernels  115 us (98%)
  local copies, waits for them, and re-layouts  1.32 us (1%)
    pallas_call x1, Pallas kernels, grid_body(): pl.pallas_call(grid_kernel, out_shape=pltpu.VMEM((vb, total_c, half, cond...  115 us

profile of v2, /device:TPU:0, one launch (start us, length us, event | category | flops | bytes accessed | tf_op | source)
XLA Modules:
  0.0 116.4 jit_solution(2156824082473591612)
XLA Ops:
  0.0 115.1 %shard_map.37 = f32[4,16,32,256]{3,2,1,0:T(8,128)S(1)} custom-call(bf16[256,4096]{1,0:T(8,128)(2,1)} %bitcast.3, bf16[256,4096]{1,0:T(8,128)(2,1)} %bitcast.4, f32[1,4096]{1,0:T(1,128)} %bitcast.5), custom_call_target="tpu_custom_call" | custom-call | tf_op jit(solution)/shard_map/pallas_call | solution.py:395
  115.1 1.3 %copy.5 = f32[4,16,32,256]{3,2,1,0:T(8,128)} copy(f32[4,16,32,256]{3,2,1,0:T(8,128)S(1)} %shard_map.37) | data formatting | bytes 4194304

commit v3 on v2

--- a/solution.py
+++ b/solution.py
@@ -9,9 +9,11 @@
 
 MESH = pl.DeviceIdType.MESH
 SIDE = 4
-CHUNKS = 8
+CHUNKS = 4
 BLOCKS = 5
 CUTS = 8
+TWICE = 1
+LAST = 16
 PARTS = 2
 
 
@@ -43,8 +45,8 @@
 
 
 def grid_kernel(
-    val, con, scr_row, out, raw, scr, bb, acc, xs, xr, zs, zr,
-    loc, a1s, a1r, a2s, a2r, a3s, a3r, b1s, b1r, b2s, b2r, b3s, b3r, b4s, b4r, gate, xss, xsr, zss, zsr,
+    val, con, scr_in, out, scr_row, raw, scr, bb, acc, xs, xr, zs, zr,
+    loc, a1s, a1r, a2s, a2r, a3s, a3r, b1s, b1r, b2s, b2r, b3s, b3r, b4s, b4r, b5s, gate, xss, xsr, zss, zsr,
 ):
     me, x = lax.axis_index("pair"), lax.axis_index("pw")
     core, y, zl, zh = me % 2, (me // 2) % 2, (me // 4) % 2, me // 8
@@ -100,8 +102,19 @@
     def b3(k):
         return remote(bit(2, k), bit(3, k), b3s.at[k], b3r.at[k], beside)
 
+    def b5(j):
+        k = bits - TWICE + j
+        return remote(bit(1, k), bit(3, k), b5s.at[j], b3r.at[k], far)
+
     def b4(k):
         return remote(bb.at[0, brows(k)], bb.at[4, brows(k)], b4s.at[k], b4r.at[k], across)
+
+    def b4_end(i):
+        low = cols - LAST
+        lines = pl.ds(cols - cstep, cstep - LAST) if i == 0 else pl.ds(low, LAST)
+        lanes = pl.ds(0, depth) if i == 0 else pl.ds((i - 1) * (depth // 2), depth // 2)
+        t = CHUNKS - 1 + i
+        return remote(bb.at[0, lines, lanes], bb.at[4, lines, lanes], b4s.at[t], b4r.at[t], across)
 
     def slot(a, b, h):
         return (b * SIDE + a) * PARTS + h
@@ -158,8 +171,11 @@
         pl.semaphore_signal(barrier, inc=1, device_id=dev, device_id_type=MESH)
     own_a = pltpu.make_async_copy(val, raw.at[0], loc.at[0])
     own_b = pltpu.make_async_copy(con, bb.at[0], loc.at[1])
+    own_row = pltpu.make_async_copy(scr_in, scr_row, loc.at[2])
+    own_row.start()
     own_a.start()
     own_b.start()
+    own_row.wait()
     own_a.wait()
     screen_all(0)
     own_b.wait()
@@ -168,7 +184,9 @@
 
     @pl.when(mid)
     def _():
-        each(CHUNKS, lambda k: b4(k).start())
+        each(CHUNKS - 1, lambda k: b4(k).start())
+        for i in range(3):
+            b4_end(i).start()
 
     each(CHUNKS, lambda k: a2(k).start())
 
@@ -254,9 +272,12 @@
     def first(k):
         @pl.when(jnp.logical_and(mid, k == CHUNKS - 1))
         def _():
-            each(CHUNKS, lambda i: b4(i).wait_send())
+            each(CHUNKS - 1, lambda i: b4(i).wait_send())
+            b4_end(0).wait_send()
+            b4_end(1).wait_send()
             for dev in (near, at(1, 0, 1, 0)):
                 pl.semaphore_signal(gate, inc=1, device_id=dev, device_id_type=MESH)
+            b4_end(2).wait_send()
 
         @pl.when(jnp.logical_and(end, k == CHUNKS - 1))
         def _():
@@ -268,7 +289,14 @@
 
         @pl.when(mid)
         def _():
-            b4(k).wait_recv()
+            @pl.when(k < CHUNKS - 1)
+            def _():
+                b4(k).wait_recv()
+
+            @pl.when(k == CHUNKS - 1)
+            def _():
+                for i in range(3):
+                    b4_end(i).wait_recv()
 
             @pl.when(k % ready == ready - 1)
             def _():
@@ -287,6 +315,13 @@
     each(PARTS * 2, lambda i: drain(1 - i // PARTS, 0, i % PARTS))
     each(CHUNKS, lambda k: b1(k).wait_recv())
 
+    @pl.when(end)
+    def _():
+        each(TWICE, lambda j: b5(j).start())
+
+    def crosses(k):
+        return jnp.logical_or(end, k < bits - TWICE)
+
     turns = 2 * SIDE
     lag = 2
 
@@ -305,7 +340,11 @@
 
     def second(k):
         b2(k).wait_recv()
-        b3(k).start()
+
+        @pl.when(crosses(k))
+        def _():
+            b3(k).start()
+
         grow(2, k)
 
         @pl.when(k < turns)
@@ -348,8 +387,8 @@
     land(1, 3, 0)
     each(4, arrive(0, 0))
     each(4, arrive(0, 1))
+    each(SIDE, lambda i: drain(SIDE - 1 - i, 3, 1))
     each(4, arrive(2, 0))
-    each(SIDE, lambda i: drain(SIDE - 1 - i, 3, 1))
     land(1, 2, 1)
     each(4, arrive(2, 1))
     land(1, 3, 1)
@@ -364,8 +403,15 @@
 
     def cleared(k):
         b2(k).wait_send()
-        b3(k).wait_send()
+
+        @pl.when(crosses(k))
+        def _():
+            b3(k).wait_send()
     each(bits, cleared)
+
+    @pl.when(end)
+    def _():
+        each(TWICE, lambda j: b5(j).wait_send())
 
     def passed(i):
         a, b, h = (i // PARTS) % SIDE, i // (PARTS * SIDE), i % PARTS
@@ -398,10 +444,11 @@
         in_specs=[
             pl.BlockSpec(memory_space=pl.ANY),
             pl.BlockSpec(memory_space=pl.ANY),
-            pl.BlockSpec(memory_space=pltpu.VMEM),
+            pl.BlockSpec(memory_space=pl.ANY),
         ],
         out_specs=pl.BlockSpec(memory_space=pltpu.VMEM),
         scratch_shapes=[
+            pltpu.VMEM((1, depth), jnp.float32),
             pltpu.VMEM((SIDE, rows, depth), bf16),
             pltpu.VMEM((SIDE, rows, depth), bf16),
             pltpu.VMEM((BLOCKS, cols, depth), bf16),
@@ -410,12 +457,13 @@
             pltpu.VMEM((tiles, vb, half, part), bf16),
             pltpu.VMEM((tiles, vb, half, part), bf16),
             pltpu.VMEM((tiles, vb, half, part), bf16),
-            dma((2,)),
+            dma((3,)),
             dma((1,)), dma((1,)),
             dma((CHUNKS,)), dma((CHUNKS,)), dma((CHUNKS,)), dma((CHUNKS,)),
             dma((CHUNKS,)), dma((CHUNKS,)),
             dma((bits,)), dma((bits,)), dma((bits,)), dma((bits,)),
-            dma((CHUNKS,)), dma((CHUNKS,)),
+            dma((CHUNKS + 2,)), dma((CHUNKS + 2,)),
+            dma((TWICE,)),
             pltpu.SemaphoreType.REGULAR,
             dma((tiles,)), dma((tiles,)), dma((tiles,)), dma((tiles,)),
         ],

time: 117 us -> 114 us (0.974)
  Pallas kernels: 115 us -> 113 us
    pallas_call x1, Pallas kernels: 115 us -> 113 us  [grid_body(): pl.pallas_call(grid_kernel, out_shape=pltpu.VMEM((vb, total_c, half, cond...]
where the time goes in v3:
time: 114 us
  Pallas kernels  113 us (99%)
  local copies, waits for them, and re-layouts  1.32 us (1%)
    pallas_call x1, Pallas kernels, grid_body(): pl.pallas_call(grid_kernel, out_shape=pltpu.VMEM((vb, total_c, half, cond...  113 us

profile of v3, /device:TPU:0, one launch (start us, length us, event | category | flops | bytes accessed | tf_op | source)
XLA Modules:
  0.0 114.1 jit_solution(8068730467855000262)
XLA Ops:
  0.0 112.8 %shard_map.37 = f32[4,16,32,256]{3,2,1,0:T(8,128)S(1)} custom-call(bf16[256,4096]{1,0:T(8,128)(2,1)} %bitcast.3, bf16[256,4096]{1,0:T(8,128)(2,1)} %bitcast.4, f32[1,4096]{1,0:T(1,128)} %bitcast.5), custom_call_target="tpu_custom_call" | custom-call | tf_op jit(solution)/shard_map/pallas_call | solution.py:441
  112.8 1.3 %copy.5 = f32[4,16,32,256]{3,2,1,0:T(8,128)} copy(f32[4,16,32,256]{3,2,1,0:T(8,128)S(1)} %shard_map.37) | data formatting | bytes 4194304

commit v4 on v3

--- a/solution.py
+++ b/solution.py
@@ -169,29 +169,43 @@
 
     for dev in greeted:
         pl.semaphore_signal(barrier, inc=1, device_id=dev, device_id_type=MESH)
-    own_a = pltpu.make_async_copy(val, raw.at[0], loc.at[0])
-    own_b = pltpu.make_async_copy(con, bb.at[0], loc.at[1])
-    own_row = pltpu.make_async_copy(scr_in, scr_row, loc.at[2])
+    def own_a(k):
+        return pltpu.make_async_copy(val.at[arows(k)], raw.at[0, arows(k)], loc.at[k])
+
+    def own_b(k):
+        return pltpu.make_async_copy(con.at[brows(k)], bb.at[0, brows(k)], loc.at[CHUNKS + k])
+
+    own_row = pltpu.make_async_copy(scr_in, scr_row, loc.at[2 * CHUNKS])
+
+    def fetch(k):
+        own_b(k).start()
+        own_a(k).start()
+
+    each(CHUNKS, fetch)
     own_row.start()
-    own_a.start()
-    own_b.start()
+    pl.semaphore_wait(barrier, len(greeted) + jnp.where(mid, 1, 0))
+
+    def open_streams(k):
+        own_b(k).wait()
+
+        @pl.when(jnp.logical_and(mid, k < CHUNKS - 1))
+        def _():
+            b4(k).start()
+
+        @pl.when(jnp.logical_and(mid, k == CHUNKS - 1))
+        def _():
+            for i in range(3):
+                b4_end(i).start()
+
+        b1(k).start()
+        own_a(k).wait()
+        a2(k).start()
+
+    each(CHUNKS, open_streams)
+    a1.start()
     own_row.wait()
-    own_a.wait()
     screen_all(0)
-    own_b.wait()
     each(2 * SIDE * PARTS, lambda i: blank(2 * SIDE * PARTS + i))
-    pl.semaphore_wait(barrier, len(greeted) + jnp.where(mid, 1, 0))
-
-    @pl.when(mid)
-    def _():
-        each(CHUNKS - 1, lambda k: b4(k).start())
-        for i in range(3):
-            b4_end(i).start()
-
-    each(CHUNKS, lambda k: a2(k).start())
-
-    each(CHUNKS, lambda k: b1(k).start())
-    a1.start()
 
     def send(a, b, h):
         @pl.when(active(a, b))
@@ -457,7 +471,7 @@
             pltpu.VMEM((tiles, vb, half, part), bf16),
             pltpu.VMEM((tiles, vb, half, part), bf16),
             pltpu.VMEM((tiles, vb, half, part), bf16),
-            dma((3,)),
+            dma((2 * CHUNKS + 1,)),
             dma((1,)), dma((1,)),
             dma((CHUNKS,)), dma((CHUNKS,)), dma((CHUNKS,)), dma((CHUNKS,)),
             dma((CHUNKS,)), dma((CHUNKS,)),

time: 114 us -> 113 us (level)
  no operation moved by 1% of the time
where the time goes in v4:
time: 113 us
  Pallas kernels  112 us (99%)
  local copies, waits for them, and re-layouts  1.32 us (1%)
    pallas_call x1, Pallas kernels, grid_body(): pl.pallas_call(grid_kernel, out_shape=pltpu.VMEM((vb, total_c, half, cond...  112 us

profile of v4, /device:TPU:0, one launch (start us, length us, event | category | flops | bytes accessed | tf_op | source)
XLA Modules:
  0.0 113.1 jit_solution(12769425187532540608)
XLA Ops:
  0.0 111.8 %shard_map.37 = f32[4,16,32,256]{3,2,1,0:T(8,128)S(1)} custom-call(bf16[256,4096]{1,0:T(8,128)(2,1)} %bitcast.3, bf16[256,4096]{1,0:T(8,128)(2,1)} %bitcast.4, f32[1,4096]{1,0:T(1,128)} %bitcast.5), custom_call_target="tpu_custom_call" | custom-call | tf_op jit(solution)/shard_map/pallas_call | solution.py:455
  111.8 1.3 %copy.5 = f32[4,16,32,256]{3,2,1,0:T(8,128)} copy(f32[4,16,32,256]{3,2,1,0:T(8,128)S(1)} %shard_map.37) | data formatting | bytes 4194304

commit v5 on v4

--- a/solution.py
+++ b/solution.py
@@ -389,7 +389,6 @@
 
     each(bits, second)
     tail(bits - 2)
-    each(SIDE, lambda i: drain(SIDE - 1 - i, 2, 1))
     tail(bits - 1)
 
     def arrive(lo, h):
@@ -397,16 +396,7 @@
             land(2 + j % 2, lo + j // 2, h)
         return one
 
-    land(1, 2, 0)
-    land(1, 3, 0)
-    each(4, arrive(0, 0))
-    each(4, arrive(0, 1))
-    each(SIDE, lambda i: drain(SIDE - 1 - i, 3, 1))
-    each(4, arrive(2, 0))
-    land(1, 2, 1)
-    each(4, arrive(2, 1))
-    land(1, 3, 1)
-
+    each(SIDE, lambda i: drain(SIDE - 1 - i, 2, 1))
     a1.wait_send()
 
     def sent(k):
@@ -437,7 +427,21 @@
             @pl.when(a > 0)
             def _():
                 zcopy(i, a).wait_send()
-    each(BLOCKS * SIDE * PARTS, passed)
+
+    land(1, 2, 0)
+    land(1, 3, 0)
+    each(SIDE, lambda i: drain(SIDE - 1 - i, 3, 1))
+    each(4, arrive(0, 0))
+    each(4, arrive(0, 1))
+    each(4, arrive(2, 0))
+    land(1, 2, 1)
+    each(2 * SIDE * PARTS, passed)
+    each(BLOCKS * SIDE * PARTS, passed, 4 * SIDE * PARTS)
+
+    each(4, arrive(2, 1))
+    land(1, 3, 1)
+
+    each(4 * SIDE * PARTS, passed, 2 * SIDE * PARTS)
 
 
 def grid_body(valence_pairs, conduction_pairs, screening):

time: 113 us -> 111 us (0.982)
  Pallas kernels: 112 us -> 110 us
    pallas_call x1, Pallas kernels: 112 us -> 110 us  [grid_body(): pl.pallas_call(grid_kernel, out_shape=pltpu.VMEM((vb, total_c, half, cond...]
where the time goes in v5:
time: 111 us
  Pallas kernels  110 us (99%)
  local copies, waits for them, and re-layouts  1.32 us (1%)
    pallas_call x1, Pallas kernels, grid_body(): pl.pallas_call(grid_kernel, out_shape=pltpu.VMEM((vb, total_c, half, cond...  110 us

profile of v5, /device:TPU:0, one launch (start us, length us, event | category | flops | bytes accessed | tf_op | source)
XLA Modules:
  0.0 111.3 jit_solution(3546092663965833325)
XLA Ops:
  0.0 109.9 %shard_map.37 = f32[4,16,32,256]{3,2,1,0:T(8,128)S(1)} custom-call(bf16[256,4096]{1,0:T(8,128)(2,1)} %bitcast.3, bf16[256,4096]{1,0:T(8,128)(2,1)} %bitcast.4, f32[1,4096]{1,0:T(1,128)} %bitcast.5), custom_call_target="tpu_custom_call" | custom-call | tf_op jit(solution)/shard_map/pallas_call | solution.py:459
  109.9 1.3 %copy.5 = f32[4,16,32,256]{3,2,1,0:T(8,128)} copy(f32[4,16,32,256]{3,2,1,0:T(8,128)S(1)} %shard_map.37) | data formatting | bytes 4194304
